TPU v7x, 32 devices: a whole 2x2x4 slice. The times are simulated.
32 devices in a mesh: group: 4 (over y, core), sub: 8 (over z, x).
Axes of the slice: x: 2, y: 2, z: 4, core: 2. Of those that a mesh axis runs over, the one named last changes fastest.
Arguments:
- shared_sizes: int32 [4, 8, 2], P('group', 'sub'), may hold values from 0 to 256, as said below
- stiffness: float32 [4, 8], P('group', 'sub'), may hold values from 0.1 to 10
- load_cases: float32 [4, 8, 1024, 384], P('group', 'sub'), may hold values from -6 to 6
- schur_blocks: bfloat16 [4, 8, 1024, 1024], P('group', 'sub')
- neumann_inverse: bfloat16 [4, 8, 1024, 1024], P('group', 'sub')
- coarse_basis: bfloat16 [4, 8, 32, 1024], P('group', 'sub'), may hold values from -0.1875 to 0.1875
- coarse_dofs: int32 [4, 8, 32], P('group', 'sub'), may hold values from 0 to 511
- coarse_inverse: float32 [512, 512], P('sub'), as said below
Outputs:
- solution: float32 [4, 8, 1024, 384], P('group', 'sub')
- residual: float32 [4, 8, 1024, 384], P('group', 'sub')
Inputs may be any that keep to these rules, and one draw needn't show every extreme that they name: shared_sizes[g, s, 0] equals shared_sizes[g, s - 1, 1]; the lower share of the first and the upper share of the last subdomain of a group are 0, the other shares lie in 128 to 256, and in every group some subdomain shares exactly 256 with its upper neighbour. `coarse_inverse`: symmetric.
All inputs are finite; a program needn't handle non-finite values.
Results may differ from a plain program's by a relative error of at most 0.0075.
Values sent between devices are 32-bit elements; how exact they have to be, the bound alone decides.
No kernel may reach another device: no remote copies, remote signals or barrier semaphores. Data moves between devices by JAX's collectives and lax.ppermute only.
A program may use at most 128 MiB of HBM per device.

v0:
```python
import jax
import jax.numpy as jnp
from jax import lax
from jax.sharding import PartitionSpec as P

MAXSH = 256
ITERS = 4
OMEGA = 0.6


def from_behind(block, axis, distance):
    devices = range(lax.axis_size(axis))
    route = [(i - distance, i) for i in devices if i - distance in devices]
    return lax.ppermute(block, axis, route)


def extended(x, sides, width):
    for axis, dim in sides:
        peers, length = (lax.axis_size(axis), x.shape[dim])
        up = [(i, (i + 1) % peers) for i in range(peers - 1)]
        down = [(j, i) for i, j in up]
        last = lax.slice_in_dim(x, length - width, length, axis=dim)
        leading = lax.slice_in_dim(x, 0, width, axis=dim)
        before = lax.ppermute(last, axis, up)
        after = lax.ppermute(leading, axis, down)
        x = jnp.concatenate([before, x, after], axis=dim)
    return x


def lift_piece(tail_rows, share_size):
    slab_width = tail_rows.shape[0]
    rolled = jnp.roll(tail_rows, share_size - slab_width, axis=0)
    inside = (jnp.arange(slab_width) < share_size)[:, None]
    return jnp.where(inside, rolled, jnp.zeros_like(rolled))


def place_piece(head_rows, share_size):
    slab_width = head_rows.shape[0]
    inside = (jnp.arange(slab_width) < share_size)[:, None]
    masked = jnp.where(inside, head_rows, jnp.zeros_like(head_rows))
    return jnp.roll(masked, slab_width - share_size, axis=0)


def assemble(vector, share_up):
    unknowns = vector.shape[0]
    tail_rows = vector[unknowns - MAXSH :]
    head_rows = vector[:MAXSH]
    lifted = lift_piece(tail_rows, share_up)
    from_lower = from_behind(lifted, "sub", 1)
    from_upper = from_behind(head_rows, "sub", -1)
    placed = place_piece(from_upper, share_up)
    return jnp.concatenate(
        [head_rows + from_lower, vector[MAXSH : unknowns - MAXSH], tail_rows + placed], axis=0
    )


def on_device(
    shared_sizes,
    stiffness,
    load_cases,
    schur_blocks,
    neumann_inverse,
    coarse_basis,
    coarse_dofs,
    coarse_inverse,
):
    share_low = shared_sizes[0, 0, 0]
    share_up = shared_sizes[0, 0, 1]
    beside_all = extended(stiffness, (("sub", 1),), 1)
    own_stiff = beside_all[0, 1]
    low_weight = own_stiff / (own_stiff + beside_all[0, 0])
    up_weight = own_stiff / (own_stiff + beside_all[0, 2])
    loads = load_cases[0, 0]
    schur = schur_blocks[0, 0]
    neumann = neumann_inverse[0, 0]
    basis = coarse_basis[0, 0]
    my_dofs = coarse_dofs[0, 0]
    unknowns, cases = loads.shape
    own_count = coarse_inverse.shape[0]
    row_index = jnp.arange(unknowns)
    weight = jnp.where(
        row_index < share_low,
        low_weight,
        jnp.where(row_index >= unknowns - share_up, up_weight, jnp.float32(1.0)),
    )[:, None]
    highest = lax.Precision.HIGHEST

    def operator_residual(solution):
        return loads - jnp.dot(
            schur, solution.astype(jnp.bfloat16), preferred_element_type=jnp.float32
        )

    solution = jnp.zeros((unknowns, cases), jnp.float32)
    for sweep in range(ITERS):
        local = operator_residual(solution)
        weighted = (weight * assemble(local, share_up)).astype(jnp.bfloat16)
        coarse_terms = jnp.dot(basis, weighted, preferred_element_type=jnp.float32)
        dof_values = my_dofs.astype(jnp.float32)
        all_terms = lax.all_gather(coarse_terms, "sub", axis=0, tiled=True)
        all_dofs = lax.all_gather(dof_values, "sub", axis=0, tiled=True)
        dof_index = all_dofs.astype(jnp.int32)
        first_row = lax.axis_index("sub") * own_count
        own_select = (dof_index[:, None] == first_row + jnp.arange(own_count)[None, :]).astype(
            jnp.float32
        )
        owned = lax.dot_general(own_select, all_terms, (((0,), (0,)), ((), ())), precision=highest)
        owned = lax.psum(owned, "group")
        columns = jnp.take(coarse_inverse, dof_index, axis=1)
        partial_vals = lax.dot_general(columns, owned, (((0,), (0,)), ((), ())), precision=highest)
        partial_vals = partial_vals.reshape(-1, coarse_terms.shape[0], cases)
        received = lax.all_to_all(partial_vals, "sub", split_axis=0, concat_axis=0, tiled=True)
        picked = jnp.sum(received, axis=0)
        picked = picked.astype(jnp.bfloat16)
        correction = jnp.dot(neumann, weighted, preferred_element_type=jnp.float32)
        correction = correction + lax.dot_general(
            basis, picked, (((0,), (0,)), ((), ())), preferred_element_type=jnp.float32
        )
        solution = solution + OMEGA * assemble(weight * correction, share_up)
    residual = assemble(operator_residual(solution), share_up)
    return (solution[None, None], residual[None, None])


def solution(mesh):
    return jax.shard_map(
        on_device,
        mesh=mesh,
        in_specs=(
            P("group", "sub", None),
            P("group", "sub"),
            P("group", "sub", None, None),
            P("group", "sub", None, None),
            P("group", "sub", None, None),
            P("group", "sub", None, None),
            P("group", "sub", None),
            P("sub", None),
        ),
        out_specs=(P("group", "sub", None, None), P("group", "sub", None, None)),
        check_vma=False,
    )
```

profile of v0, /device:TPU:16, one launch (start us, length us, event | category | flops | bytes accessed | tf_op | source)
XLA Modules:
  0.0 597.5 jit_solution(9661922671992732006)
XLA Ops:
  7.2 3.4 collective-permute-start.1
  20.8 4.2 collective-permute-start.3
  31.0 14.9 %all-reduce = f32[256]{0:T(256)S(1)} all-reduce(f32[256]{0:T(256)S(1)} %bitcast_dynamic-update-slice_fusion), channel_id=2, replica_groups=mesh['group'=4,'sub'=8] {'sub'}, use_global_device_ids=true, to_apply=%add | all-reduce | flops 256 | bytes 2048
  54.6 6.0 %collective-permute-done.2 = f32[256,384]{0,1:T(8,128)} collective-permute-done((f32[256,384]{0,1:T(8,128)}, f32[256,384]{0,1:T(8,128)}, u32[]{:S(2)}, u32[]{:S(2)}) %collective-permute-start.2) | collective-permute-done | bytes 393248 | tf_op jit(solution)/shard_map/ppermute | solution.py:14
  63.2 27.9 %all_gather.19 = f32[256,384]{1,0:T(8,128)S(1)} all-gather(f32[32,384]{1,0:T(8,128)S(1)} %convolution_bitcast_fusion.3), channel_id=1, replica_groups=mesh['group'=4,'sub'=8] {'sub'}, dimensions={0}, use_global_device_ids=true | all-gather | bytes 442368 | tf_op jit(solution)/shard_map/all_gather | solution.py:99
  93.1 34.8 %all-reduce.6.cloned.1.call-done = f32[64,384]{1,0:T(8,128)} async-done(((f32[64,384]{1,0:T(8,128)}), f32[64,384]{1,0:T(8,128)}) %all-reduce.6.cloned.1.call-update) | async-done | bytes 98320 | tf_op jit(solution)/shard_map/psum | solution.py:107
  129.4 15.0 %all_to_all.20 = f32[8,32,384]{2,1,0:T(8,128)} all-to-all(f32[8,32,384]{2,1,0:T(8,128)S(1)} %bitcast.145), channel_id=1, replica_groups=mesh['group'=4,'sub'=8] {'sub'}, dimensions={0} | all-to-all | bytes 786432 | tf_op jit(solution)/shard_map/all_to_all | solution.py:111
  152.3 8.6 %collective-permute-done.5 = f32[256,384]{0,1:T(8,128)S(1)} collective-permute-done((f32[256,384]{0,1:T(8,128)S(1)}, f32[256,384]{0,1:T(8,128)S(1)}, u32[]{:S(2)}, u32[]{:S(2)}) %collective-permute-start.5) | collective-permute-done | bytes 393248 | tf_op jit(solution)/shard_map/ppermute | solution.py:14
  165.2 7.9 %collective-permute-done.4 = f32[256,384]{0,1:T(8,128)S(1)} collective-permute-done((f32[256,384]{0,1:T(8,128)S(1)}, f32[256,384]{0,1:T(8,128)S(1)}, u32[]{:S(2)}, u32[]{:S(2)}) %collective-permute-start.4) | collective-permute-done | bytes 393248 | tf_op jit(solution)/shard_map/ppermute | solution.py:14
  176.5 8.2 %collective-permute-done.7 = f32[256,384]{0,1:T(8,128)S(1)} collective-permute-done((f32[256,384]{0,1:T(8,128)S(1)}, f32[256,384]{0,1:T(8,128)S(1)}, u32[]{:S(2)}, u32[]{:S(2)}) %collective-permute-start.7) | collective-permute-done | bytes 393248 | tf_op jit(solution)/shard_map/ppermute | solution.py:14
  187.6 8.1 %collective-permute-done.6 = f32[256,384]{0,1:T(8,128)S(1)} collective-permute-done((f32[256,384]{0,1:T(8,128)S(1)}, f32[256,384]{0,1:T(8,128)S(1)}, u32[]{:S(2)}, u32[]{:S(2)}) %collective-permute-start.6) | collective-permute-done | bytes 393248 | tf_op jit(solution)/shard_map/ppermute | solution.py:14
  196.3 25.4 %all_gather.20 = f32[256,384]{1,0:T(8,128)S(1)} all-gather(f32[32,384]{1,0:T(8,128)S(1)} %convolution_bitcast_fusion.2), channel_id=1, replica_groups=mesh['group'=4,'sub'=8] {'sub'}, dimensions={0}, use_global_device_ids=true | all-gather | bytes 442368 | tf_op jit(solution)/shard_map/all_gather | solution.py:99
  222.8 34.4 %all-reduce.8.cloned.1.call-done = f32[64,384]{1,0:T(8,128)} async-done(((f32[64,384]{1,0:T(8,128)}), f32[64,384]{1,0:T(8,128)}) %all-reduce.8.cloned.1.call-update) | async-done | bytes 98320 | tf_op jit(solution)/shard_map/psum | solution.py:107
  258.6 14.9 %all_to_all.21 = f32[8,32,384]{2,1,0:T(8,128)} all-to-all(f32[8,32,384]{2,1,0:T(8,128)S(1)} %bitcast.146), channel_id=1, replica_groups=mesh['group'=4,'sub'=8] {'sub'}, dimensions={0} | all-to-all | bytes 786432 | tf_op jit(solution)/shard_map/all_to_all | solution.py:111
  281.7 8.6 %collective-permute-done.9 = f32[256,384]{0,1:T(8,128)S(1)} collective-permute-done((f32[256,384]{0,1:T(8,128)S(1)}, f32[256,384]{0,1:T(8,128)S(1)}, u32[]{:S(2)}, u32[]{:S(2)}) %collective-permute-start.9) | collective-permute-done | bytes 393248 | tf_op jit(solution)/shard_map/ppermute | solution.py:14
  294.9 7.6 %collective-permute-done.8 = f32[256,384]{0,1:T(8,128)S(1)} collective-permute-done((f32[256,384]{0,1:T(8,128)S(1)}, f32[256,384]{0,1:T(8,128)S(1)}, u32[]{:S(2)}, u32[]{:S(2)}) %collective-permute-start.8) | collective-permute-done | bytes 393248 | tf_op jit(solution)/shard_map/ppermute | solution.py:14
  305.9 8.2 %collective-permute-done.11 = f32[256,384]{0,1:T(8,128)S(1)} collective-permute-done((f32[256,384]{0,1:T(8,128)S(1)}, f32[256,384]{0,1:T(8,128)S(1)}, u32[]{:S(2)}, u32[]{:S(2)}) %collective-permute-start.11) | collective-permute-done | bytes 393248 | tf_op jit(solution)/shard_map/ppermute | solution.py:14
  317.0 8.0 %collective-permute-done.10 = f32[256,384]{0,1:T(8,128)S(1)} collective-permute-done((f32[256,384]{0,1:T(8,128)S(1)}, f32[256,384]{0,1:T(8,128)S(1)}, u32[]{:S(2)}, u32[]{:S(2)}) %collective-permute-start.10) | collective-permute-done | bytes 393248 | tf_op jit(solution)/shard_map/ppermute | solution.py:14
  325.7 25.4 %all_gather.21 = f32[256,384]{1,0:T(8,128)S(1)} all-gather(f32[32,384]{1,0:T(8,128)S(1)} %convolution_bitcast_fusion.1), channel_id=1, replica_groups=mesh['group'=4,'sub'=8] {'sub'}, dimensions={0}, use_global_device_ids=true | all-gather | bytes 442368 | tf_op jit(solution)/shard_map/all_gather | solution.py:99
  352.2 34.4 %all-reduce.10.cloned.1.call-done = f32[64,384]{1,0:T(8,128)} async-done(((f32[64,384]{1,0:T(8,128)}), f32[64,384]{1,0:T(8,128)}) %all-reduce.10.cloned.1.call-update) | async-done | bytes 98320 | tf_op jit(solution)/shard_map/psum | solution.py:107
  388.0 14.9 %all_to_all.22 = f32[8,32,384]{2,1,0:T(8,128)} all-to-all(f32[8,32,384]{2,1,0:T(8,128)S(1)} %bitcast.147), channel_id=1, replica_groups=mesh['group'=4,'sub'=8] {'sub'}, dimensions={0} | all-to-all | bytes 786432 | tf_op jit(solution)/shard_map/all_to_all | solution.py:111
  411.1 8.6 %collective-permute-done.13 = f32[256,384]{0,1:T(8,128)S(1)} collective-permute-done((f32[256,384]{0,1:T(8,128)S(1)}, f32[256,384]{0,1:T(8,128)S(1)}, u32[]{:S(2)}, u32[]{:S(2)}) %collective-permute-start.13) | collective-permute-done | bytes 393248 | tf_op jit(solution)/shard_map/ppermute | solution.py:14
  424.0 7.9 %collective-permute-done.12 = f32[256,384]{0,1:T(8,128)S(1)} collective-permute-done((f32[256,384]{0,1:T(8,128)S(1)}, f32[256,384]{0,1:T(8,128)S(1)}, u32[]{:S(2)}, u32[]{:S(2)}) %collective-permute-start.12) | collective-permute-done | bytes 393248 | tf_op jit(solution)/shard_map/ppermute | solution.py:14
  435.4 8.2 %collective-permute-done.15 = f32[256,384]{0,1:T(8,128)S(1)} collective-permute-done((f32[256,384]{0,1:T(8,128)S(1)}, f32[256,384]{0,1:T(8,128)S(1)}, u32[]{:S(2)}, u32[]{:S(2)}) %collective-permute-start.15) | collective-permute-done | bytes 393248 | tf_op jit(solution)/shard_map/ppermute | solution.py:14
  446.5 8.1 %collective-permute-done.14 = f32[256,384]{0,1:T(8,128)S(1)} collective-permute-done((f32[256,384]{0,1:T(8,128)S(1)}, f32[256,384]{0,1:T(8,128)S(1)}, u32[]{:S(2)}, u32[]{:S(2)}) %collective-permute-start.14) | collective-permute-done | bytes 393248 | tf_op jit(solution)/shard_map/ppermute | solution.py:14
  455.2 25.4 %all_gather.22 = f32[256,384]{1,0:T(8,128)S(1)} all-gather(f32[32,384]{1,0:T(8,128)S(1)} %convolution_bitcast_fusion), channel_id=1, replica_groups=mesh['group'=4,'sub'=8] {'sub'}, dimensions={0}, use_global_device_ids=true | all-gather | bytes 442368 | tf_op jit(solution)/shard_map/all_gather | solution.py:99
  481.6 34.4 %all-reduce.12.cloned.1.call-done = f32[64,384]{1,0:T(8,128)} async-done(((f32[64,384]{1,0:T(8,128)}), f32[64,384]{1,0:T(8,128)}) %all-reduce.12.cloned.1.call-update) | async-done | bytes 98320 | tf_op jit(solution)/shard_map/psum | solution.py:107
  517.5 14.9 %all_to_all.23 = f32[8,32,384]{2,1,0:T(8,128)} all-to-all(f32[8,32,384]{2,1,0:T(8,128)S(1)} %bitcast.144), channel_id=1, replica_groups=mesh['group'=4,'sub'=8] {'sub'}, dimensions={0} | all-to-all | bytes 786432 | tf_op jit(solution)/shard_map/all_to_all | solution.py:111
  540.6 8.6 %collective-permute-done.17 = f32[256,384]{0,1:T(8,128)S(1)} collective-permute-done((f32[256,384]{0,1:T(8,128)S(1)}, f32[256,384]{0,1:T(8,128)S(1)}, u32[]{:S(2)}, u32[]{:S(2)}) %collective-permute-start.17) | collective-permute-done | bytes 393248 | tf_op jit(solution)/shard_map/ppermute | solution.py:14
  552.6 8.7 %collective-permute-done.16 = f32[256,384]{0,1:T(8,128)S(1)} collective-permute-done((f32[256,384]{0,1:T(8,128)S(1)}, f32[256,384]{0,1:T(8,128)S(1)}, u32[]{:S(2)}, u32[]{:S(2)}) %collective-permute-start.16) | collective-permute-done | bytes 393248 | tf_op jit(solution)/shard_map/ppermute | solution.py:14
  565.0 8.2 %collective-permute-done.19 = f32[256,384]{0,1:T(8,128)S(1)} collective-permute-done((f32[256,384]{0,1:T(8,128)S(1)}, f32[256,384]{0,1:T(8,128)S(1)}, u32[]{:S(2)}, u32[]{:S(2)}) %collective-permute-start.19) | collective-permute-done | bytes 393248 | tf_op jit(solution)/shard_map/ppermute | solution.py:14
  581.5 3.6 collective-permute-done.18
  (215 shorter events, 120.2 us)
Async XLA Ops:
  7.2 120.8 %all-reduce.6.cloned.1.call-start = ((), (), s32[]{:S(2)}) async-start(), calls=%async_computation.4 | async-start | bytes 196608 | tf_op jit(solution)/shard_map/psum | solution.py:107
  7.2 45.2 %collective-permute-start.1 = (f32[1,1]{1,0:T(1,128)}, f32[1,1]{1,0:T(1,128)}, u32[]{:S(2)}, u32[]{:S(2)}) collective-permute-start(f32[1,1]{1,0:T(1,128)} %param.13), channel_id=1, source_target_pairs={{1,0},{2,1},{3,2},{4,3},{5,4},{6,5},{7,6},{9,8},{10,9},{11,10},{12... | collective-permute-start | bytes 20 | tf_op jit(solution)/shard_map/ppermute | solution.py:25
  10.7 42.5 %collective-permute-start = (f32[1,1]{1,0:T(1,128)}, f32[1,1]{1,0:T(1,128)}, u32[]{:S(2)}, u32[]{:S(2)}) collective-permute-start(f32[1,1]{1,0:T(1,128)} %param.13), channel_id=1, source_target_pairs={{0,1},{1,2},{2,3},{3,4},{4,5},{5,6},{6,7},{8,9},{9,10},{10,11},{11... | collective-permute-start | bytes 20 | tf_op jit(solution)/shard_map/ppermute | solution.py:24
  20.8 25.8 %collective-permute-start.3 = (f32[256,384]{0,1:T(8,128)}, f32[256,384]{0,1:T(8,128)S(1)}, u32[]{:S(2)}, u32[]{:S(2)}) collective-permute-start(f32[256,384]{0,1:T(8,128)} %get-tuple-element.51), channel_id=1, source_target_pairs={{1,0},{2,1},{3,2},{4,3},{5,4},{6,5},{7,6},{9,8},{10,9},{11,10},{12... | collective-permute-start | bytes 1179656 | tf_op jit(solution)/shard_map/ppermute | solution.py:14
  49.6 13.3 %copy-start.40 = (bf16[1,1,32,1024]{3,2,1,0:T(8,128)(2,1)S(1)}, bf16[1,1,32,1024]{3,2,1,0:T(8,128)(2,1)}, u32[]{:S(2)}) copy-start(bf16[1,1,32,1024]{3,2,1,0:T(8,128)(2,1)} %param.17) | copy-start | bytes 196612
  49.6 11.0 %collective-permute-start.2 = (f32[256,384]{0,1:T(8,128)}, f32[256,384]{0,1:T(8,128)}, u32[]{:S(2)}, u32[]{:S(2)}) collective-permute-start(f32[256,384]{0,1:T(8,128)} %get-tuple-element.70), channel_id=1, source_target_pairs={{0,1},{1,2},{2,3},{3,4},{4,5},{5,6},{6,7},{8,9},{9,10},{10,11},{11... | collective-permute-start | bytes 1179656 | tf_op jit(solution)/shard_map/ppermute | solution.py:14
  62.8 29.4 %copy-start.47 = (f32[64,512]{1,0:T(8,128)S(1)}, f32[64,512]{1,0:T(8,128)}, u32[]{:S(2)}) copy-start(f32[64,512]{1,0:T(8,128)} %param.19) | copy-start | bytes 393220
  92.2 165.0 %all-reduce.8.cloned.1.call-start = ((), (), s32[]{:S(2)}) async-start(), calls=%async_computation.5 | async-start | bytes 196608 | tf_op jit(solution)/shard_map/psum | solution.py:107
  129.4 16.4 %copy-start.21 = (f32[256,384]{0,1:T(8,128)S(1)}, f32[256,384]{0,1:T(8,128)}, u32[]{:S(2)}) copy-start(f32[256,384]{0,1:T(8,128)} %copy-done.20) | copy-start | bytes 1179652
  149.1 11.8 %collective-permute-start.5 = (f32[256,384]{0,1:T(8,128)S(1)}, f32[256,384]{0,1:T(8,128)S(1)}, u32[]{:S(2)}, u32[]{:S(2)}) collective-permute-start(f32[256,384]{0,1:T(8,128)S(1)} %get-tuple-element.47), channel_id=1, source_target_pairs={{1,0},{2,1},{3,2},{4,3},{5,4},{6,5},{7,6},{9,8},{10,9},{11,10},{12... | collective-permute-start | bytes 1179656 | tf_op jit(solution)/shard_map/ppermute | solution.py:14
  161.2 11.9 %collective-permute-start.4 = (f32[256,384]{0,1:T(8,128)S(1)}, f32[256,384]{0,1:T(8,128)S(1)}, u32[]{:S(2)}, u32[]{:S(2)}) collective-permute-start(f32[256,384]{0,1:T(8,128)S(1)} %get-tuple-element.66), channel_id=1, source_target_pairs={{0,1},{1,2},{2,3},{3,4},{4,5},{5,6},{6,7},{8,9},{9,10},{10,11},{11... | collective-permute-start | bytes 1179656 | tf_op jit(solution)/shard_map/ppermute | solution.py:14
  174.6 10.1 %collective-permute-start.7 = (f32[256,384]{0,1:T(8,128)S(1)}, f32[256,384]{0,1:T(8,128)S(1)}, u32[]{:S(2)}, u32[]{:S(2)}) collective-permute-start(f32[256,384]{0,1:T(8,128)S(1)} %get-tuple-element.41), channel_id=1, source_target_pairs={{1,0},{2,1},{3,2},{4,3},{5,4},{6,5},{7,6},{9,8},{10,9},{11,10},{12... | collective-permute-start | bytes 1179656 | tf_op jit(solution)/shard_map/ppermute | solution.py:14
  185.0 10.7 %collective-permute-start.6 = (f32[256,384]{0,1:T(8,128)S(1)}, f32[256,384]{0,1:T(8,128)S(1)}, u32[]{:S(2)}, u32[]{:S(2)}) collective-permute-start(f32[256,384]{0,1:T(8,128)S(1)} %get-tuple-element.64), channel_id=1, source_target_pairs={{0,1},{1,2},{2,3},{3,4},{4,5},{5,6},{6,7},{8,9},{9,10},{10,11},{11... | collective-permute-start | bytes 1179656 | tf_op jit(solution)/shard_map/ppermute | solution.py:14
  195.9 25.8 %copy-start.26 = (f32[256,384]{0,1:T(8,128)}, f32[256,384]{0,1:T(8,128)S(1)}, u32[]{:S(2)}) copy-start(f32[256,384]{0,1:T(8,128)S(1)} %get-tuple-element.39) | copy-start | bytes 1179652
  222.7 163.8 %all-reduce.10.cloned.1.call-start = ((), (), s32[]{:S(2)}) async-start(), calls=%async_computation.6 | async-start | bytes 196608 | tf_op jit(solution)/shard_map/psum | solution.py:107
  278.5 11.8 %collective-permute-start.9 = (f32[256,384]{0,1:T(8,128)S(1)}, f32[256,384]{0,1:T(8,128)S(1)}, u32[]{:S(2)}, u32[]{:S(2)}) collective-permute-start(f32[256,384]{0,1:T(8,128)S(1)} %get-tuple-element.37), channel_id=1, source_target_pairs={{1,0},{2,1},{3,2},{4,3},{5,4},{6,5},{7,6},{9,8},{10,9},{11,10},{12... | collective-permute-start | bytes 1179656 | tf_op jit(solution)/shard_map/ppermute | solution.py:14
  290.6 11.9 %collective-permute-start.8 = (f32[256,384]{0,1:T(8,128)S(1)}, f32[256,384]{0,1:T(8,128)S(1)}, u32[]{:S(2)}, u32[]{:S(2)}) collective-permute-start(f32[256,384]{0,1:T(8,128)S(1)} %get-tuple-element.62), channel_id=1, source_target_pairs={{0,1},{1,2},{2,3},{3,4},{4,5},{5,6},{6,7},{8,9},{9,10},{10,11},{11... | collective-permute-start | bytes 1179656 | tf_op jit(solution)/shard_map/ppermute | solution.py:14
  303.9 10.1 %collective-permute-start.11 = (f32[256,384]{0,1:T(8,128)S(1)}, f32[256,384]{0,1:T(8,128)S(1)}, u32[]{:S(2)}, u32[]{:S(2)}) collective-permute-start(f32[256,384]{0,1:T(8,128)S(1)} %get-tuple-element.31), channel_id=1, source_target_pairs={{1,0},{2,1},{3,2},{4,3},{5,4},{6,5},{7,6},{9,8},{10,9},{11,10},{12... | collective-permute-start | bytes 1179656 | tf_op jit(solution)/shard_map/ppermute | solution.py:14
  314.3 10.7 %collective-permute-start.10 = (f32[256,384]{0,1:T(8,128)S(1)}, f32[256,384]{0,1:T(8,128)S(1)}, u32[]{:S(2)}, u32[]{:S(2)}) collective-permute-start(f32[256,384]{0,1:T(8,128)S(1)} %get-tuple-element.60), channel_id=1, source_target_pairs={{0,1},{1,2},{2,3},{3,4},{4,5},{5,6},{6,7},{8,9},{9,10},{10,11},{11... | collective-permute-start | bytes 1179656 | tf_op jit(solution)/shard_map/ppermute | solution.py:14
  325.3 25.8 %copy-start.28 = (f32[256,384]{0,1:T(8,128)}, f32[256,384]{0,1:T(8,128)S(1)}, u32[]{:S(2)}) copy-start(f32[256,384]{0,1:T(8,128)S(1)} %get-tuple-element.29) | copy-start | bytes 1179652
  352.1 163.9 %all-reduce.12.cloned.1.call-start = ((), (), s32[]{:S(2)}) async-start(), calls=%async_computation.7 | async-start | bytes 196608 | tf_op jit(solution)/shard_map/psum | solution.py:107
  407.9 11.9 %collective-permute-start.13 = (f32[256,384]{0,1:T(8,128)S(1)}, f32[256,384]{0,1:T(8,128)S(1)}, u32[]{:S(2)}, u32[]{:S(2)}) collective-permute-start(f32[256,384]{0,1:T(8,128)S(1)} %get-tuple-element.27), channel_id=1, source_target_pairs={{1,0},{2,1},{3,2},{4,3},{5,4},{6,5},{7,6},{9,8},{10,9},{11,10},{12... | collective-permute-start | bytes 1179656 | tf_op jit(solution)/shard_map/ppermute | solution.py:14
  420.0 11.9 %collective-permute-start.12 = (f32[256,384]{0,1:T(8,128)S(1)}, f32[256,384]{0,1:T(8,128)S(1)}, u32[]{:S(2)}, u32[]{:S(2)}) collective-permute-start(f32[256,384]{0,1:T(8,128)S(1)} %get-tuple-element.58), channel_id=1, source_target_pairs={{0,1},{1,2},{2,3},{3,4},{4,5},{5,6},{6,7},{8,9},{9,10},{10,11},{11... | collective-permute-start | bytes 1179656 | tf_op jit(solution)/shard_map/ppermute | solution.py:14
  433.4 10.1 %collective-permute-start.15 = (f32[256,384]{0,1:T(8,128)S(1)}, f32[256,384]{0,1:T(8,128)S(1)}, u32[]{:S(2)}, u32[]{:S(2)}) collective-permute-start(f32[256,384]{0,1:T(8,128)S(1)} %get-tuple-element.21), channel_id=1, source_target_pairs={{1,0},{2,1},{3,2},{4,3},{5,4},{6,5},{7,6},{9,8},{10,9},{11,10},{12... | collective-permute-start | bytes 1179656 | tf_op jit(solution)/shard_map/ppermute | solution.py:14
  443.9 10.7 %collective-permute-start.14 = (f32[256,384]{0,1:T(8,128)S(1)}, f32[256,384]{0,1:T(8,128)S(1)}, u32[]{:S(2)}, u32[]{:S(2)}) collective-permute-start(f32[256,384]{0,1:T(8,128)S(1)} %get-tuple-element.56), channel_id=1, source_target_pairs={{0,1},{1,2},{2,3},{3,4},{4,5},{5,6},{6,7},{8,9},{9,10},{10,11},{11... | collective-permute-start | bytes 1179656 | tf_op jit(solution)/shard_map/ppermute | solution.py:14
  454.8 25.8 %copy-start.24 = (f32[256,384]{0,1:T(8,128)}, f32[256,384]{0,1:T(8,128)S(1)}, u32[]{:S(2)}) copy-start(f32[256,384]{0,1:T(8,128)S(1)} %get-tuple-element.19) | copy-start | bytes 1179652
  537.3 11.8 %collective-permute-start.17 = (f32[256,384]{0,1:T(8,128)S(1)}, f32[256,384]{0,1:T(8,128)S(1)}, u32[]{:S(2)}, u32[]{:S(2)}) collective-permute-start(f32[256,384]{0,1:T(8,128)S(1)} %get-tuple-element.17), channel_id=1, source_target_pairs={{1,0},{2,1},{3,2},{4,3},{5,4},{6,5},{7,6},{9,8},{10,9},{11,10},{12... | collective-permute-start | bytes 1179656 | tf_op jit(solution)/shard_map/ppermute | solution.py:14
  549.2 12.5 %copy-start.45 = (f32[512,384]{0,1:T(8,128)S(1)}, f32[512,384]{0,1:T(8,128)}, u32[]{:S(2)}) copy-start(f32[512,384]{0,1:T(8,128)} %copy-done.44) | copy-start | bytes 2359300
  549.5 11.9 %collective-permute-start.16 = (f32[256,384]{0,1:T(8,128)S(1)}, f32[256,384]{0,1:T(8,128)S(1)}, u32[]{:S(2)}, u32[]{:S(2)}) collective-permute-start(f32[256,384]{0,1:T(8,128)S(1)} %get-tuple-element.54), channel_id=1, source_target_pairs={{0,1},{1,2},{2,3},{3,4},{4,5},{5,6},{6,7},{8,9},{9,10},{10,11},{11... | collective-permute-start | bytes 1179656 | tf_op jit(solution)/shard_map/ppermute | solution.py:14
  563.0 13.8 %copy-start.6 = (f32[1024,384]{0,1:T(8,128)}, f32[1024,384]{0,1:T(8,128)S(1)}, u32[]{:S(2)}) copy-start(f32[1024,384]{0,1:T(8,128)S(1)} %bitcast_subtract_fusion) | copy-start | bytes 4718596
  563.1 10.1 %collective-permute-start.19 = (f32[256,384]{0,1:T(8,128)S(1)}, f32[256,384]{0,1:T(8,128)S(1)}, u32[]{:S(2)}, u32[]{:S(2)}) collective-permute-start(f32[256,384]{0,1:T(8,128)S(1)} %get-tuple-element.11), channel_id=1, source_target_pairs={{1,0},{2,1},{3,2},{4,3},{5,4},{6,5},{7,6},{9,8},{10,9},{11,10},{12... | collective-permute-start | bytes 1179656 | tf_op jit(solution)/shard_map/ppermute | solution.py:14
  574.3 10.9 %collective-permute-start.18 = (f32[256,384]{0,1:T(8,128)}, f32[256,384]{0,1:T(8,128)}, u32[]{:S(2)}, u32[]{:S(2)}) collective-permute-start(f32[256,384]{0,1:T(8,128)} %get-tuple-element.52), channel_id=1, source_target_pairs={{0,1},{1,2},{2,3},{3,4},{4,5},{5,6},{6,7},{8,9},{9,10},{10,11},{11... | collective-permute-start | bytes 1179656 | tf_op jit(solution)/shard_map/ppermute | solution.py:14
  (44 other events, 245.8 us)
Sparse Core Ops, SparseCore 0:
  92.3 35.5 all-reduce.5
  222.9 34.2 all-reduce.7
  352.2 34.2 all-reduce.9
  481.7 34.2 all-reduce.11
where the time goes:
time: 599 us; the launch traced here: 598 us
  waiting for transfers between devices  271 us (45%)
  blocking collectives  179 us (30%)
  starting transfers between devices  55.8 us (9%)
  matrix products  30 us (5%)
  local copies, waits for them, and re-layouts  23.2 us (4%)
  between operations  19.8 us (3%)
  other arithmetic  18.8 us (3%)
    psum x4, waiting for transfers between devices, on_device(): owned = lax.psum(owned, 'group')  138 us
    ppermute x18, waiting for transfers between devices, from_behind(): return lax.ppermute(block, axis, route)  133 us
    all_gather x4, blocking collectives, on_device(): all_terms = lax.all_gather(coarse_terms, 'sub', axis=0, tiled=True)  104 us
    all_to_all x4, blocking collectives, on_device(): lax.all_to_all(partial_vals, 'sub', split_axis=0, concat_axis=0, tiled=True)  59.6 us
    ppermute x18, starting transfers between devices, from_behind(): return lax.ppermute(block, axis, route)  49.6 us
    unnamed x108, local copies, waits for them, and re-layouts  15.7 us
    unnamed x1, blocking collectives  14.9 us
  transfers between devices with their start and end apart: 24, of which 21 were waited for; matrix products, arithmetic and copies ran while one was open for 4% of the time, Pallas kernels for 0%

commit v1 on v0

--- a/solution.py
+++ b/solution.py
@@ -6,6 +6,15 @@
 MAXSH = 256
 ITERS = 4
 OMEGA = 0.6
+
+
+def add_in_pairs(x, mesh_axis):
+    peers = lax.axis_size(mesh_axis)
+    result, reach = (x, 1)
+    while reach < peers:
+        result = result + lax.ppermute(result, mesh_axis, [(i, i ^ reach) for i in range(peers)])
+        reach = 2 * reach
+    return result
 
 
 def from_behind(block, axis, distance):
@@ -104,7 +113,7 @@
             jnp.float32
         )
         owned = lax.dot_general(own_select, all_terms, (((0,), (0,)), ((), ())), precision=highest)
-        owned = lax.psum(owned, "group")
+        owned = add_in_pairs(owned, "group")
         columns = jnp.take(coarse_inverse, dof_index, axis=1)
         partial_vals = lax.dot_general(columns, owned, (((0,), (0,)), ((), ())), precision=highest)
         partial_vals = partial_vals.reshape(-1, coarse_terms.shape[0], cases)

time: 599 us -> 482 us (0.80)
  waiting for transfers between devices: 271 us -> 150 us
  blocking collectives: 179 us -> 194 us
  between operations: 19.8 us -> 6.26 us
  starting transfers between devices: 55.8 us -> 64 us
    psum x4 -> x0, waiting for transfers between devices: 138 us -> none  [on_device(): owned = lax.psum(owned, 'group')]
    ppermute x0 -> x8, waiting for transfers between devices: none -> 17.3 us  [add_in_pairs(): lax.ppermute(result, mesh_axis, [(i, i ^ reach) for i in range(peers)])]
    all_to_all x4, blocking collectives: 59.6 us -> 72.6 us  [on_device(): lax.all_to_all(partial_vals, 'sub', split_axis=0, concat_axis=0, tiled=True)]
    ppermute x0 -> x8, starting transfers between devices: none -> 7.19 us  [add_in_pairs(): lax.ppermute(result, mesh_axis, [(i, i ^ reach) for i in range(peers)])]
  transfers between devices with their start and end apart: 24 -> 28, of which waited for: 21 -> 25; matrix products, arithmetic and copies ran while one was open for 4% -> 4% of each run, Pallas kernels for 0% -> 0%
where the time goes in v1:
time: 482 us; the launch traced here: 480 us
  blocking collectives  194 us (40%)
  waiting for transfers between devices  150 us (31%)
  starting transfers between devices  64 us (13%)
  matrix products  24.7 us (5%)
  local copies, waits for them, and re-layouts  22.4 us (5%)
  other arithmetic  19.6 us (4%)
  between operations  6.26 us (1%)
    ppermute x18, waiting for transfers between devices, from_behind(): return lax.ppermute(block, axis, route)  132 us
    all_gather x4, blocking collectives, on_device(): all_terms = lax.all_gather(coarse_terms, 'sub', axis=0, tiled=True)  106 us
    all_to_all x4, blocking collectives, on_device(): lax.all_to_all(partial_vals, 'sub', split_axis=0, concat_axis=0, tiled=True)  72.6 us
    ppermute x18, starting transfers between devices, from_behind(): return lax.ppermute(block, axis, route)  50.9 us
    ppermute x8, waiting for transfers between devices, add_in_pairs(): lax.ppermute(result, mesh_axis, [(i, i ^ reach) for i in range(peers)])  17.3 us
    unnamed x108, local copies, waits for them, and re-layouts  15 us
    unnamed x1, blocking collectives  14.8 us
    dot_general x4, matrix products, on_device(): correction = jnp.dot(neumann, weighted, preferred_element_type=jnp.float32)  10.6 us
  transfers between devices with their start and end apart: 28, of which 25 were waited for; matrix products, arithmetic and copies ran while one was open for 4% of the time, Pallas kernels for 0%

profile of v1, /device:TPU:16, one launch (start us, length us, event | category | flops | bytes accessed | tf_op | source)
XLA Modules:
  0.0 480.1 jit_solution(12757094747064048575)
XLA Ops:
  0.6 3.4 collective-permute-start.1
  14.2 4.2 collective-permute-start.3
  24.0 14.8 %all-reduce = f32[256]{0:T(256)S(1)} all-reduce(f32[256]{0:T(256)S(1)} %bitcast_dynamic-update-slice_fusion), channel_id=2, replica_groups=mesh['group'=4,'sub'=8] {'sub'}, use_global_device_ids=true, to_apply=%add | all-reduce | flops 256 | bytes 2048
  47.2 6.2 %collective-permute-done.2 = f32[256,384]{0,1:T(8,128)} collective-permute-done((f32[256,384]{0,1:T(8,128)}, f32[256,384]{0,1:T(8,128)}, u32[]{:S(2)}, u32[]{:S(2)}) %collective-permute-start.2) | collective-permute-done | bytes 393248 | tf_op jit(solution)/shard_map/ppermute | solution.py:23
  55.3 28.0 %all_gather.19 = f32[256,384]{1,0:T(8,128)S(1)} all-gather(f32[32,384]{1,0:T(8,128)S(1)} %convolution_bitcast_fusion.3), channel_id=1, replica_groups=mesh['group'=4,'sub'=8] {'sub'}, dimensions={0}, use_global_device_ids=true | all-gather | bytes 442368 | tf_op jit(solution)/shard_map/all_gather | solution.py:108
  92.6 18.8 %all_to_all.20 = f32[8,32,384]{2,1,0:T(8,128)} all-to-all(f32[8,32,384]{2,1,0:T(8,128)S(1)} %bitcast.141), channel_id=1, replica_groups=mesh['group'=4,'sub'=8] {'sub'}, dimensions={0} | all-to-all | bytes 786432 | tf_op jit(solution)/shard_map/all_to_all | solution.py:120
  116.1 3.2 collective-permute-start.7
  119.3 8.6 %collective-permute-done.7 = f32[256,384]{0,1:T(8,128)S(1)} collective-permute-done((f32[256,384]{0,1:T(8,128)S(1)}, f32[256,384]{0,1:T(8,128)S(1)}, u32[]{:S(2)}, u32[]{:S(2)}) %collective-permute-start.7) | collective-permute-done | bytes 393248 | tf_op jit(solution)/shard_map/ppermute | solution.py:23
  132.3 7.9 %collective-permute-done.6 = f32[256,384]{0,1:T(8,128)S(1)} collective-permute-done((f32[256,384]{0,1:T(8,128)S(1)}, f32[256,384]{0,1:T(8,128)S(1)}, u32[]{:S(2)}, u32[]{:S(2)}) %collective-permute-start.6) | collective-permute-done | bytes 393248 | tf_op jit(solution)/shard_map/ppermute | solution.py:23
  143.5 8.2 %collective-permute-done.9 = f32[256,384]{0,1:T(8,128)S(1)} collective-permute-done((f32[256,384]{0,1:T(8,128)S(1)}, f32[256,384]{0,1:T(8,128)S(1)}, u32[]{:S(2)}, u32[]{:S(2)}) %collective-permute-start.9) | collective-permute-done | bytes 393248 | tf_op jit(solution)/shard_map/ppermute | solution.py:23
  154.7 7.9 %collective-permute-done.8 = f32[256,384]{0,1:T(8,128)S(1)} collective-permute-done((f32[256,384]{0,1:T(8,128)S(1)}, f32[256,384]{0,1:T(8,128)S(1)}, u32[]{:S(2)}, u32[]{:S(2)}) %collective-permute-start.8) | collective-permute-done | bytes 393248 | tf_op jit(solution)/shard_map/ppermute | solution.py:23
  163.3 26.1 %all_gather.20 = f32[256,384]{1,0:T(8,128)S(1)} all-gather(f32[32,384]{1,0:T(8,128)S(1)} %convolution_bitcast_fusion.2), channel_id=1, replica_groups=mesh['group'=4,'sub'=8] {'sub'}, dimensions={0}, use_global_device_ids=true | all-gather | bytes 442368 | tf_op jit(solution)/shard_map/all_gather | solution.py:108
  196.6 17.9 %all_to_all.21 = f32[8,32,384]{2,1,0:T(8,128)} all-to-all(f32[8,32,384]{2,1,0:T(8,128)S(1)} %bitcast.142), channel_id=1, replica_groups=mesh['group'=4,'sub'=8] {'sub'}, dimensions={0} | all-to-all | bytes 786432 | tf_op jit(solution)/shard_map/all_to_all | solution.py:120
  219.5 3.3 collective-permute-start.13
  222.7 8.6 %collective-permute-done.13 = f32[256,384]{0,1:T(8,128)S(1)} collective-permute-done((f32[256,384]{0,1:T(8,128)S(1)}, f32[256,384]{0,1:T(8,128)S(1)}, u32[]{:S(2)}, u32[]{:S(2)}) %collective-permute-start.13) | collective-permute-done | bytes 393248 | tf_op jit(solution)/shard_map/ppermute | solution.py:23
  235.9 7.6 %collective-permute-done.12 = f32[256,384]{0,1:T(8,128)S(1)} collective-permute-done((f32[256,384]{0,1:T(8,128)S(1)}, f32[256,384]{0,1:T(8,128)S(1)}, u32[]{:S(2)}, u32[]{:S(2)}) %collective-permute-start.12) | collective-permute-done | bytes 393248 | tf_op jit(solution)/shard_map/ppermute | solution.py:23
  246.9 8.2 %collective-permute-done.15 = f32[256,384]{0,1:T(8,128)S(1)} collective-permute-done((f32[256,384]{0,1:T(8,128)S(1)}, f32[256,384]{0,1:T(8,128)S(1)}, u32[]{:S(2)}, u32[]{:S(2)}) %collective-permute-start.15) | collective-permute-done | bytes 393248 | tf_op jit(solution)/shard_map/ppermute | solution.py:23
  258.2 7.9 %collective-permute-done.14 = f32[256,384]{0,1:T(8,128)S(1)} collective-permute-done((f32[256,384]{0,1:T(8,128)S(1)}, f32[256,384]{0,1:T(8,128)S(1)}, u32[]{:S(2)}, u32[]{:S(2)}) %collective-permute-start.14) | collective-permute-done | bytes 393248 | tf_op jit(solution)/shard_map/ppermute | solution.py:23
  266.7 25.9 %all_gather.21 = f32[256,384]{1,0:T(8,128)S(1)} all-gather(f32[32,384]{1,0:T(8,128)S(1)} %convolution_bitcast_fusion.1), channel_id=1, replica_groups=mesh['group'=4,'sub'=8] {'sub'}, dimensions={0}, use_global_device_ids=true | all-gather | bytes 442368 | tf_op jit(solution)/shard_map/all_gather | solution.py:108
  299.9 18.0 %all_to_all.22 = f32[8,32,384]{2,1,0:T(8,128)} all-to-all(f32[8,32,384]{2,1,0:T(8,128)S(1)} %bitcast.143), channel_id=1, replica_groups=mesh['group'=4,'sub'=8] {'sub'}, dimensions={0} | all-to-all | bytes 786432 | tf_op jit(solution)/shard_map/all_to_all | solution.py:120
  322.9 3.2 collective-permute-start.19
  326.1 8.6 %collective-permute-done.19 = f32[256,384]{0,1:T(8,128)S(1)} collective-permute-done((f32[256,384]{0,1:T(8,128)S(1)}, f32[256,384]{0,1:T(8,128)S(1)}, u32[]{:S(2)}, u32[]{:S(2)}) %collective-permute-start.19) | collective-permute-done | bytes 393248 | tf_op jit(solution)/shard_map/ppermute | solution.py:23
  339.1 7.8 %collective-permute-done.18 = f32[256,384]{0,1:T(8,128)S(1)} collective-permute-done((f32[256,384]{0,1:T(8,128)S(1)}, f32[256,384]{0,1:T(8,128)S(1)}, u32[]{:S(2)}, u32[]{:S(2)}) %collective-permute-start.18) | collective-permute-done | bytes 393248 | tf_op jit(solution)/shard_map/ppermute | solution.py:23
  350.4 8.2 %collective-permute-done.21 = f32[256,384]{0,1:T(8,128)S(1)} collective-permute-done((f32[256,384]{0,1:T(8,128)S(1)}, f32[256,384]{0,1:T(8,128)S(1)}, u32[]{:S(2)}, u32[]{:S(2)}) %collective-permute-start.21) | collective-permute-done | bytes 393248 | tf_op jit(solution)/shard_map/ppermute | solution.py:23
  361.6 7.9 %collective-permute-done.20 = f32[256,384]{0,1:T(8,128)S(1)} collective-permute-done((f32[256,384]{0,1:T(8,128)S(1)}, f32[256,384]{0,1:T(8,128)S(1)}, u32[]{:S(2)}, u32[]{:S(2)}) %collective-permute-start.20) | collective-permute-done | bytes 393248 | tf_op jit(solution)/shard_map/ppermute | solution.py:23
  370.2 26.1 %all_gather.22 = f32[256,384]{1,0:T(8,128)S(1)} all-gather(f32[32,384]{1,0:T(8,128)S(1)} %convolution_bitcast_fusion), channel_id=1, replica_groups=mesh['group'=4,'sub'=8] {'sub'}, dimensions={0}, use_global_device_ids=true | all-gather | bytes 442368 | tf_op jit(solution)/shard_map/all_gather | solution.py:108
  403.5 17.9 %all_to_all.23 = f32[8,32,384]{2,1,0:T(8,128)} all-to-all(f32[8,32,384]{2,1,0:T(8,128)S(1)} %bitcast.140), channel_id=1, replica_groups=mesh['group'=4,'sub'=8] {'sub'}, dimensions={0} | all-to-all | bytes 786432 | tf_op jit(solution)/shard_map/all_to_all | solution.py:120
  426.4 3.3 collective-permute-start.25
  429.7 8.6 %collective-permute-done.25 = f32[256,384]{0,1:T(8,128)S(1)} collective-permute-done((f32[256,384]{0,1:T(8,128)S(1)}, f32[256,384]{0,1:T(8,128)S(1)}, u32[]{:S(2)}, u32[]{:S(2)}) %collective-permute-start.25) | collective-permute-done | bytes 393248 | tf_op jit(solution)/shard_map/ppermute | solution.py:23
  442.0 8.5 %collective-permute-done.24 = f32[256,384]{0,1:T(8,128)S(1)} collective-permute-done((f32[256,384]{0,1:T(8,128)S(1)}, f32[256,384]{0,1:T(8,128)S(1)}, u32[]{:S(2)}, u32[]{:S(2)}) %collective-permute-start.24) | collective-permute-done | bytes 393248 | tf_op jit(solution)/shard_map/ppermute | solution.py:23
  454.1 8.2 %collective-permute-done.27 = f32[256,384]{0,1:T(8,128)S(1)} collective-permute-done((f32[256,384]{0,1:T(8,128)S(1)}, f32[256,384]{0,1:T(8,128)S(1)}, u32[]{:S(2)}, u32[]{:S(2)}) %collective-permute-start.27) | collective-permute-done | bytes 393248 | tf_op jit(solution)/shard_map/ppermute | solution.py:23
  470.8 3.5 collective-permute-done.26
  (223 shorter events, 127.4 us)
Async XLA Ops:
  0.6 44.6 %collective-permute-start.1 = (f32[1,1]{1,0:T(1,128)}, f32[1,1]{1,0:T(1,128)}, u32[]{:S(2)}, u32[]{:S(2)}) collective-permute-start(f32[1,1]{1,0:T(1,128)} %param.13), channel_id=1, source_target_pairs={{1,0},{2,1},{3,2},{4,3},{5,4},{6,5},{7,6},{9,8},{10,9},{11,10},{12... | collective-permute-start | bytes 20 | tf_op jit(solution)/shard_map/ppermute | solution.py:34
  4.1 41.8 %collective-permute-start = (f32[1,1]{1,0:T(1,128)}, f32[1,1]{1,0:T(1,128)}, u32[]{:S(2)}, u32[]{:S(2)}) collective-permute-start(f32[1,1]{1,0:T(1,128)} %param.13), channel_id=1, source_target_pairs={{0,1},{1,2},{2,3},{3,4},{4,5},{5,6},{6,7},{8,9},{9,10},{10,11},{11... | collective-permute-start | bytes 20 | tf_op jit(solution)/shard_map/ppermute | solution.py:33
  14.2 25.2 %collective-permute-start.3 = (f32[256,384]{0,1:T(8,128)}, f32[256,384]{0,1:T(8,128)S(1)}, u32[]{:S(2)}, u32[]{:S(2)}) collective-permute-start(f32[256,384]{0,1:T(8,128)} %get-tuple-element.51), channel_id=1, source_target_pairs={{1,0},{2,1},{3,2},{4,3},{5,4},{6,5},{7,6},{9,8},{10,9},{11,10},{12... | collective-permute-start | bytes 1179656 | tf_op jit(solution)/shard_map/ppermute | solution.py:23
  42.4 11.0 %collective-permute-start.2 = (f32[256,384]{0,1:T(8,128)}, f32[256,384]{0,1:T(8,128)}, u32[]{:S(2)}, u32[]{:S(2)}) collective-permute-start(f32[256,384]{0,1:T(8,128)} %get-tuple-element.70), channel_id=1, source_target_pairs={{0,1},{1,2},{2,3},{3,4},{4,5},{5,6},{6,7},{8,9},{9,10},{10,11},{11... | collective-permute-start | bytes 1179656 | tf_op jit(solution)/shard_map/ppermute | solution.py:23
  54.9 28.8 %copy-start.20 = (f32[256,384]{0,1:T(8,128)}, f32[256,384]{0,1:T(8,128)S(1)}, u32[]{:S(2)}) copy-start(f32[256,384]{0,1:T(8,128)S(1)} %get-tuple-element.48) | copy-start | bytes 1179652
  54.9 28.8 %copy-start.22 = (f32[256,384]{0,1:T(8,128)}, f32[256,384]{0,1:T(8,128)S(1)}, u32[]{:S(2)}) copy-start(f32[256,384]{0,1:T(8,128)S(1)} %get-tuple-element.49) | copy-start | bytes 1179652
  55.0 28.9 %copy-start.47 = (f32[64,512]{1,0:T(8,128)S(1)}, f32[64,512]{1,0:T(8,128)}, u32[]{:S(2)}) copy-start(f32[64,512]{1,0:T(8,128)} %param.19) | copy-start | bytes 393220
  83.7 1.5 collective-permute-start.4
  86.1 5.0 %collective-permute-start.5 = (f32[64,384]{1,0:T(8,128)S(1)}, f32[64,384]{1,0:T(8,128)}, u32[]{:S(2)}, u32[]{:S(2)}) collective-permute-start(f32[64,384]{1,0:T(8,128)S(1)} %add.174), channel_id=1, source_target_pairs={{0,16},{8,24},{16,0},{24,8},{1,17},{9,25},{17,1},{25,9},{2,18},{10... | collective-permute-start | bytes 294920 | tf_op jit(solution)/shard_map/ppermute | solution.py:15
  116.1 11.9 %collective-permute-start.7 = (f32[256,384]{0,1:T(8,128)S(1)}, f32[256,384]{0,1:T(8,128)S(1)}, u32[]{:S(2)}, u32[]{:S(2)}) collective-permute-start(f32[256,384]{0,1:T(8,128)S(1)} %get-tuple-element.47), channel_id=1, source_target_pairs={{1,0},{2,1},{3,2},{4,3},{5,4},{6,5},{7,6},{9,8},{10,9},{11,10},{12... | collective-permute-start | bytes 1179656 | tf_op jit(solution)/shard_map/ppermute | solution.py:23
  128.2 11.9 %collective-permute-start.6 = (f32[256,384]{0,1:T(8,128)S(1)}, f32[256,384]{0,1:T(8,128)S(1)}, u32[]{:S(2)}, u32[]{:S(2)}) collective-permute-start(f32[256,384]{0,1:T(8,128)S(1)} %get-tuple-element.66), channel_id=1, source_target_pairs={{0,1},{1,2},{2,3},{3,4},{4,5},{5,6},{6,7},{8,9},{9,10},{10,11},{11... | collective-permute-start | bytes 1179656 | tf_op jit(solution)/shard_map/ppermute | solution.py:23
  141.5 10.1 %collective-permute-start.9 = (f32[256,384]{0,1:T(8,128)S(1)}, f32[256,384]{0,1:T(8,128)S(1)}, u32[]{:S(2)}, u32[]{:S(2)}) collective-permute-start(f32[256,384]{0,1:T(8,128)S(1)} %get-tuple-element.41), channel_id=1, source_target_pairs={{1,0},{2,1},{3,2},{4,3},{5,4},{6,5},{7,6},{9,8},{10,9},{11,10},{12... | collective-permute-start | bytes 1179656 | tf_op jit(solution)/shard_map/ppermute | solution.py:23
  152.0 10.7 %collective-permute-start.8 = (f32[256,384]{0,1:T(8,128)S(1)}, f32[256,384]{0,1:T(8,128)S(1)}, u32[]{:S(2)}, u32[]{:S(2)}) collective-permute-start(f32[256,384]{0,1:T(8,128)S(1)} %get-tuple-element.64), channel_id=1, source_target_pairs={{0,1},{1,2},{2,3},{3,4},{4,5},{5,6},{6,7},{8,9},{9,10},{10,11},{11... | collective-permute-start | bytes 1179656 | tf_op jit(solution)/shard_map/ppermute | solution.py:23
  189.8 1.4 collective-permute-start.10
  191.1 4.9 %collective-permute-start.11 = (f32[64,384]{1,0:T(8,128)S(1)}, f32[64,384]{1,0:T(8,128)S(1)}, u32[]{:S(2)}, u32[]{:S(2)}) collective-permute-start(f32[64,384]{1,0:T(8,128)S(1)} %add.181), channel_id=1, source_target_pairs={{0,16},{8,24},{16,0},{24,8},{1,17},{9,25},{17,1},{25,9},{2,18},{10... | collective-permute-start | bytes 294920 | tf_op jit(solution)/shard_map/ppermute | solution.py:15
  219.5 11.9 %collective-permute-start.13 = (f32[256,384]{0,1:T(8,128)S(1)}, f32[256,384]{0,1:T(8,128)S(1)}, u32[]{:S(2)}, u32[]{:S(2)}) collective-permute-start(f32[256,384]{0,1:T(8,128)S(1)} %get-tuple-element.37), channel_id=1, source_target_pairs={{1,0},{2,1},{3,2},{4,3},{5,4},{6,5},{7,6},{9,8},{10,9},{11,10},{12... | collective-permute-start | bytes 1179656 | tf_op jit(solution)/shard_map/ppermute | solution.py:23
  231.6 11.9 %collective-permute-start.12 = (f32[256,384]{0,1:T(8,128)S(1)}, f32[256,384]{0,1:T(8,128)S(1)}, u32[]{:S(2)}, u32[]{:S(2)}) collective-permute-start(f32[256,384]{0,1:T(8,128)S(1)} %get-tuple-element.62), channel_id=1, source_target_pairs={{0,1},{1,2},{2,3},{3,4},{4,5},{5,6},{6,7},{8,9},{9,10},{10,11},{11... | collective-permute-start | bytes 1179656 | tf_op jit(solution)/shard_map/ppermute | solution.py:23
  245.0 10.1 %collective-permute-start.15 = (f32[256,384]{0,1:T(8,128)S(1)}, f32[256,384]{0,1:T(8,128)S(1)}, u32[]{:S(2)}, u32[]{:S(2)}) collective-permute-start(f32[256,384]{0,1:T(8,128)S(1)} %get-tuple-element.31), channel_id=1, source_target_pairs={{1,0},{2,1},{3,2},{4,3},{5,4},{6,5},{7,6},{9,8},{10,9},{11,10},{12... | collective-permute-start | bytes 1179656 | tf_op jit(solution)/shard_map/ppermute | solution.py:23
  255.4 10.7 %collective-permute-start.14 = (f32[256,384]{0,1:T(8,128)S(1)}, f32[256,384]{0,1:T(8,128)S(1)}, u32[]{:S(2)}, u32[]{:S(2)}) collective-permute-start(f32[256,384]{0,1:T(8,128)S(1)} %get-tuple-element.60), channel_id=1, source_target_pairs={{0,1},{1,2},{2,3},{3,4},{4,5},{5,6},{6,7},{8,9},{9,10},{10,11},{11... | collective-permute-start | bytes 1179656 | tf_op jit(solution)/shard_map/ppermute | solution.py:23
  293.1 1.4 collective-permute-start.16
  294.4 4.9 %collective-permute-start.17 = (f32[64,384]{1,0:T(8,128)S(1)}, f32[64,384]{1,0:T(8,128)S(1)}, u32[]{:S(2)}, u32[]{:S(2)}) collective-permute-start(f32[64,384]{1,0:T(8,128)S(1)} %add.190), channel_id=1, source_target_pairs={{0,16},{8,24},{16,0},{24,8},{1,17},{9,25},{17,1},{25,9},{2,18},{10... | collective-permute-start | bytes 294920 | tf_op jit(solution)/shard_map/ppermute | solution.py:15
  322.9 11.9 %collective-permute-start.19 = (f32[256,384]{0,1:T(8,128)S(1)}, f32[256,384]{0,1:T(8,128)S(1)}, u32[]{:S(2)}, u32[]{:S(2)}) collective-permute-start(f32[256,384]{0,1:T(8,128)S(1)} %get-tuple-element.27), channel_id=1, source_target_pairs={{1,0},{2,1},{3,2},{4,3},{5,4},{6,5},{7,6},{9,8},{10,9},{11,10},{12... | collective-permute-start | bytes 1179656 | tf_op jit(solution)/shard_map/ppermute | solution.py:23
  335.0 11.9 %collective-permute-start.18 = (f32[256,384]{0,1:T(8,128)S(1)}, f32[256,384]{0,1:T(8,128)S(1)}, u32[]{:S(2)}, u32[]{:S(2)}) collective-permute-start(f32[256,384]{0,1:T(8,128)S(1)} %get-tuple-element.58), channel_id=1, source_target_pairs={{0,1},{1,2},{2,3},{3,4},{4,5},{5,6},{6,7},{8,9},{9,10},{10,11},{11... | collective-permute-start | bytes 1179656 | tf_op jit(solution)/shard_map/ppermute | solution.py:23
  348.4 10.1 %collective-permute-start.21 = (f32[256,384]{0,1:T(8,128)S(1)}, f32[256,384]{0,1:T(8,128)S(1)}, u32[]{:S(2)}, u32[]{:S(2)}) collective-permute-start(f32[256,384]{0,1:T(8,128)S(1)} %get-tuple-element.21), channel_id=1, source_target_pairs={{1,0},{2,1},{3,2},{4,3},{5,4},{6,5},{7,6},{9,8},{10,9},{11,10},{12... | collective-permute-start | bytes 1179656 | tf_op jit(solution)/shard_map/ppermute | solution.py:23
  358.9 10.7 %collective-permute-start.20 = (f32[256,384]{0,1:T(8,128)S(1)}, f32[256,384]{0,1:T(8,128)S(1)}, u32[]{:S(2)}, u32[]{:S(2)}) collective-permute-start(f32[256,384]{0,1:T(8,128)S(1)} %get-tuple-element.56), channel_id=1, source_target_pairs={{0,1},{1,2},{2,3},{3,4},{4,5},{5,6},{6,7},{8,9},{9,10},{10,11},{11... | collective-permute-start | bytes 1179656 | tf_op jit(solution)/shard_map/ppermute | solution.py:23
  369.8 26.9 %copy-start.24 = (f32[256,384]{0,1:T(8,128)}, f32[256,384]{0,1:T(8,128)S(1)}, u32[]{:S(2)}) copy-start(f32[256,384]{0,1:T(8,128)S(1)} %get-tuple-element.19) | copy-start | bytes 1179652
  396.7 1.4 collective-permute-start.22
  398.1 4.9 %collective-permute-start.23 = (f32[64,384]{1,0:T(8,128)S(1)}, f32[64,384]{1,0:T(8,128)S(1)}, u32[]{:S(2)}, u32[]{:S(2)}) collective-permute-start(f32[64,384]{1,0:T(8,128)S(1)} %add.199), channel_id=1, source_target_pairs={{0,16},{8,24},{16,0},{24,8},{1,17},{9,25},{17,1},{25,9},{2,18},{10... | collective-permute-start | bytes 294920 | tf_op jit(solution)/shard_map/ppermute | solution.py:15
  426.4 11.9 %collective-permute-start.25 = (f32[256,384]{0,1:T(8,128)S(1)}, f32[256,384]{0,1:T(8,128)S(1)}, u32[]{:S(2)}, u32[]{:S(2)}) collective-permute-start(f32[256,384]{0,1:T(8,128)S(1)} %get-tuple-element.17), channel_id=1, source_target_pairs={{1,0},{2,1},{3,2},{4,3},{5,4},{6,5},{7,6},{9,8},{10,9},{11,10},{12... | collective-permute-start | bytes 1179656 | tf_op jit(solution)/shard_map/ppermute | solution.py:23
  438.5 11.9 %collective-permute-start.24 = (f32[256,384]{0,1:T(8,128)S(1)}, f32[256,384]{0,1:T(8,128)S(1)}, u32[]{:S(2)}, u32[]{:S(2)}) collective-permute-start(f32[256,384]{0,1:T(8,128)S(1)} %get-tuple-element.54), channel_id=1, source_target_pairs={{0,1},{1,2},{2,3},{3,4},{4,5},{5,6},{6,7},{8,9},{9,10},{10,11},{11... | collective-permute-start | bytes 1179656 | tf_op jit(solution)/shard_map/ppermute | solution.py:23
  452.2 10.1 %collective-permute-start.27 = (f32[256,384]{0,1:T(8,128)S(1)}, f32[256,384]{0,1:T(8,128)S(1)}, u32[]{:S(2)}, u32[]{:S(2)}) collective-permute-start(f32[256,384]{0,1:T(8,128)S(1)} %get-tuple-element.11), channel_id=1, source_target_pairs={{1,0},{2,1},{3,2},{4,3},{5,4},{6,5},{7,6},{9,8},{10,9},{11,10},{12... | collective-permute-start | bytes 1179656 | tf_op jit(solution)/shard_map/ppermute | solution.py:23
  463.3 10.9 %collective-permute-start.26 = (f32[256,384]{0,1:T(8,128)}, f32[256,384]{0,1:T(8,128)}, u32[]{:S(2)}, u32[]{:S(2)}) collective-permute-start(f32[256,384]{0,1:T(8,128)} %get-tuple-element.52), channel_id=1, source_target_pairs={{0,1},{1,2},{2,3},{3,4},{4,5},{5,6},{6,7},{8,9},{9,10},{10,11},{11... | collective-permute-start | bytes 1179656 | tf_op jit(solution)/shard_map/ppermute | solution.py:23
  (48 other events, 361.0 us)
